TPU v7x, 32 devices: a whole 2x2x4 slice. The times are simulated.
32 devices in a mesh: gx: 4 (over x, core), gy: 2 (over y), gz: 4 (over z).
Axes of the slice: x: 2, y: 2, z: 4, core: 2. Of those that a mesh axis runs over, the one named last changes fastest.
Arguments:
- warped_image: float32 [256, 128, 512], P('gx', 'gy', 'gz'), may hold values from -6 to 6
- fixed_image: float32 [256, 128, 512], P('gx', 'gy', 'gz'), may hold values from -6 to 6
- fine_control: float32 [3, 32, 16, 64], P(None, 'gx', 'gy', 'gz'), may hold values from -6 to 6
- coarse_control: float32 [3, 8, 4, 16], replicated, may hold values from -6 to 6
Outputs:
- fine_gradient: float32 [3, 32, 16, 64], P(None, 'gx', 'gy', 'gz')
- coarse_gradient: float32 [3, 8, 4, 16], replicated
All inputs are finite; a program needn't handle non-finite values.
Results may differ from a plain program's by a relative error of at most 0.0003.
Values sent between devices are 32-bit elements; how exact they have to be, the bound alone decides.
A program may use at most 64 MiB of HBM per device.

v0:
```python
import jax
import jax.numpy as jnp
from jax import lax
from jax.sharding import PartitionSpec as P

SPF = 8
SPC = 32
bend_factor = 0.01
highest = lax.Precision.HIGHEST


def padded_2(block, sides, width):
    for axis, dim in sides:
        count = lax.axis_size(axis)
        forward = [(i, i + 1) for i in range(count - 1)]
        backward = [(target, source) for source, target in forward]
        low = lax.ppermute(
            lax.slice_in_dim(block, block.shape[dim] - width, None, axis=dim), axis, forward
        )
        high = lax.ppermute(lax.slice_in_dim(block, 0, width, axis=dim), axis, backward)
        block = jnp.concatenate([low, block, high], axis=dim)
    return block


def spline(values):
    magnitude = jnp.abs(values)
    inner = 2.0 / 3.0 - magnitude * magnitude + 0.5 * magnitude * magnitude * magnitude
    remain = 2.0 - magnitude
    outer = remain * remain * remain / 6.0
    return jnp.where(magnitude < 1.0, inner, jnp.where(magnitude < 2.0, outer, 0.0 * magnitude))


def basis_matrix(voxels, points, spacing, voxel_start, point_start):
    voxel = (jnp.arange(voxels, dtype=jnp.int32) + voxel_start).astype(jnp.float32) + 0.5
    centre = (jnp.arange(points, dtype=jnp.int32) + point_start).astype(
        jnp.float32
    ) * spacing + 0.5 * spacing
    return spline((voxel[:, None] - centre[None, :]) / spacing)


def slope(padded, axis):
    rank = padded.ndim
    count = padded.shape[axis] - 4

    def shifted(offset):
        piece = lax.slice_in_dim(padded, offset, offset + count, axis=axis)
        for other in range(rank - 3, rank):
            if other != axis:
                piece = lax.slice_in_dim(piece, 2, piece.shape[other] - 2, axis=other)
        return piece

    return (shifted(0) - 8.0 * shifted(1) + 8.0 * shifted(3) - shifted(4)) / 12.0


def stencil(padded):
    centre = padded[:, 1:-1, 1:-1, 1:-1]
    total = padded[:, 2:, 1:-1, 1:-1] + padded[:, :-2, 1:-1, 1:-1]
    total = total + padded[:, 1:-1, 2:, 1:-1] + padded[:, 1:-1, :-2, 1:-1]
    total = total + padded[:, 1:-1, 1:-1, 2:] + padded[:, 1:-1, 1:-1, :-2]
    return total - 6.0 * centre


def laplace(field):
    return stencil(jnp.pad(field, ((0, 0), (1, 1), (1, 1), (1, 1))))


def project(force, along_x, along_y, along_z):
    section = jnp.einsum("axyz,xp->apyz", force, along_x, precision=highest)
    section = jnp.einsum("apyz,yq->apqz", section, along_y, precision=highest)
    return jnp.einsum("apqz,zr->apqr", section, along_z, precision=highest)


def settle(extended, axis, points):
    own_part = lax.slice_in_dim(extended, 4, points + 4, axis=axis)
    from_left = lax.slice_in_dim(extended, 0, 2, axis=axis)
    from_right = lax.slice_in_dim(extended, points + 6, points + 8, axis=axis)
    leading = [(0, 0)] * extended.ndim
    trailing = [(0, 0)] * extended.ndim
    leading[axis] = (0, points - 2)
    trailing[axis] = (points - 2, 0)
    return own_part + jnp.pad(from_left, leading) + jnp.pad(from_right, trailing)


def inside(position, points, devices):
    global_index = position * points - 1 + jnp.arange(points + 2, dtype=jnp.int32)
    return ((global_index >= 0) & (global_index < points * devices)).astype(jnp.float32)


def per_device(warped_image, fixed_image, fine_control, coarse_control):
    size_x, size_y, size_z = warped_image.shape
    difference = warped_image - fixed_image
    padded = padded_2(warped_image + fixed_image, (("gx", 0), ("gy", 1), ("gz", 2)), 2)
    slopes = [0.5 * slope(padded, axis) for axis in range(3)]
    force = jnp.stack(slopes) * difference[None]
    points_x = size_x // SPF
    points_y = size_y // SPF
    points_z = size_z // SPF
    part = project(
        force,
        basis_matrix(size_x, points_x + 4, SPF, 0, -2),
        basis_matrix(size_y, points_y + 4, SPF, 0, -2),
        basis_matrix(size_z, points_z + 4, SPF, 0, -2),
    )
    part = settle(padded_2(part, (("gx", 1),), 2), 1, points_x)
    part = settle(padded_2(part, (("gy", 2),), 2), 2, points_y)
    part = settle(padded_2(part, (("gz", 3),), 2), 3, points_z)
    control = padded_2(fine_control, (("gx", 1), ("gy", 2), ("gz", 3)), 2)
    first = stencil(control)
    valid_x = inside(lax.axis_index("gx"), points_x, lax.axis_size("gx"))
    valid_y = inside(lax.axis_index("gy"), points_y, lax.axis_size("gy"))
    valid_z = inside(lax.axis_index("gz"), points_z, lax.axis_size("gz"))
    region = valid_x[:, None, None] * valid_y[None, :, None] * valid_z[None, None, :]
    first = first * region[None]
    fine_gradient = part * SPF ** (-1.5) + bend_factor * stencil(first)
    coarse_x = basis_matrix(size_x, coarse_control.shape[1], SPC, lax.axis_index("gx") * size_x, 0)
    coarse_y = basis_matrix(size_y, coarse_control.shape[2], SPC, lax.axis_index("gy") * size_y, 0)
    coarse_z = basis_matrix(size_z, coarse_control.shape[3], SPC, lax.axis_index("gz") * size_z, 0)
    coarse_part = project(force, coarse_x, coarse_y, coarse_z)
    coarse_sum = lax.psum(coarse_part, ("gx", "gy", "gz"))
    coarse_gradient = coarse_sum * SPC ** (-1.5) + bend_factor * laplace(laplace(coarse_control))
    return (fine_gradient, coarse_gradient)


def solution(mesh):
    in_specs = (P("gx", "gy", "gz"), P("gx", "gy", "gz"), P(None, "gx", "gy", "gz"), P())
    out_specs = (P(None, "gx", "gy", "gz"), P())
    return jax.shard_map(
        per_device, mesh=mesh, in_specs=in_specs, out_specs=out_specs, check_vma=False
    )
```

profile of v0, /device:TPU:0, one launch (start us, length us, event | category | flops | bytes accessed | tf_op | source)
XLA Modules:
  0.0 158.9 jit_solution(8543917966219928136)
XLA Ops:
  0.7 4.4 %fusion.237 = (f32[64,64,128]{2,1,0:T(8,128)}, f32[64,64,128]{2,1,0:T(8,128)S(1)}) fusion(f32[64,64,128]{2,1,0:T(8,128)} %param.4, f32[64,64,128]{2,1,0:T(8,128)} %param.5), kind=kLoop, calls=%fused_computation.303 | loop fusion | flops 1048576 | bytes 8388608 | tf_op jit(solution)/shard_map/sub | solution.py:91
  5.1 2.4 %collective-permute-start = (f32[2,64,128]{2,1,0:T(8,128)S(1)}, f32[2,64,128]{2,1,0:T(8,128)S(1)}, u32[]{:S(2)}, u32[]{:S(2)}) collective-permute-start(f32[2,64,128]{2,1,0:T(8,128)S(1)} %get-tuple-element.16), channel_id=1, source_target_pairs={{0,8},{8,16},{16,24},{1,9},{9,17},{17,25},{2,10},{10,18},{18,26},{... | collective-permute-start | bytes 196616 | tf_op jit(solution)/shard_map/ppermute | solution.py:17
  7.5 1.3 collective-permute-start.1
  8.8 5.1 %collective-permute-start.12 = (f32[3,2,8,16]{3,2,1,0:T(8,128)S(1)}, f32[3,2,8,16]{3,2,1,0:T(8,128)S(1)}, u32[]{:S(2)}, u32[]{:S(2)}) collective-permute-start(f32[3,2,8,16]{3,2,1,0:T(8,128)S(1)} %get-tuple-element.29), channel_id=1, source_target_pairs={{0,8},{8,16},{16,24},{1,9},{9,17},{17,25},{2,10},{10,18},{18,26},{... | collective-permute-start | bytes 9224 | tf_op jit(solution)/shard_map/ppermute | solution.py:17
  14.0 1.3 collective-permute-start.13
  15.7 2.6 %collective-permute-done.13 = f32[3,2,8,16]{3,2,1,0:T(8,128)S(1)} collective-permute-done((f32[3,2,8,16]{3,2,1,0:T(8,128)S(1)}, f32[3,2,8,16]{3,2,1,0:T(8,128)S(1)}, u32[]{:S(2)}, u32[]{:S(2)}) %collective-permute-start.13) | collective-permute-done | bytes 3104 | tf_op jit(solution)/shard_map/ppermute | solution.py:20
  18.3 3.4 %collective-permute-start.14 = (f32[3,12,2,16]{3,2,1,0:T(2,128)S(1)}, f32[3,12,2,16]{3,2,1,0:T(2,128)S(1)}, u32[]{:S(2)}, u32[]{:S(2)}) collective-permute-start(f32[3,12,2,16]{3,2,1,0:T(2,128)S(1)} %get-tuple-element.24), channel_id=1, source_target_pairs={{0,4},{1,5},{2,6},{3,7},{8,12},{9,13},{10,14},{11,15},{16,20},{17,... | collective-permute-start | bytes 13832 | tf_op jit(solution)/shard_map/ppermute | solution.py:17
  21.8 1.3 collective-permute-start.15
  23.1 0.3 collective-permute-done.14
  23.4 4.2 %collective-permute-done.15 = f32[3,12,2,16]{3,2,1,0:T(2,128)S(1)} collective-permute-done((f32[3,12,2,16]{3,2,1,0:T(2,128)S(1)}, f32[3,12,2,16]{3,2,1,0:T(2,128)S(1)}, u32[]{:S(2)}, u32[]{:S(2)}) %collective-permute-start.15) | collective-permute-done | bytes 4640 | tf_op jit(solution)/shard_map/ppermute | solution.py:20
  27.8 3.5 %collective-permute-start.16 = (f32[3,12,12,2]{3,2,1,0:T(8,128)S(1)}, f32[3,12,12,2]{3,2,1,0:T(8,128)S(1)}, u32[]{:S(2)}, u32[]{:S(2)}) collective-permute-start(f32[3,12,12,2]{3,2,1,0:T(8,128)S(1)} %get-tuple-element.20), channel_id=1, source_target_pairs={{0,1},{1,2},{2,3},{4,5},{5,6},{6,7},{8,9},{9,10},{10,11},{12,13},{... | collective-permute-start | bytes 10376 | tf_op jit(solution)/shard_map/ppermute | solution.py:17
  31.3 1.3 collective-permute-start.17
  32.7 5.9 %collective-permute-done.16 = f32[3,12,12,2]{3,2,1,0:T(8,128)S(1)} collective-permute-done((f32[3,12,12,2]{3,2,1,0:T(8,128)S(1)}, f32[3,12,12,2]{3,2,1,0:T(8,128)S(1)}, u32[]{:S(2)}, u32[]{:S(2)}) %collective-permute-start.16) | collective-permute-done | bytes 3488 | tf_op jit(solution)/shard_map/ppermute | solution.py:17
  38.5 4.4 %collective-permute-done.17 = f32[3,12,12,2]{3,2,1,0:T(8,128)S(1)} collective-permute-done((f32[3,12,12,2]{3,2,1,0:T(8,128)S(1)}, f32[3,12,12,2]{3,2,1,0:T(8,128)S(1)}, u32[]{:S(2)}, u32[]{:S(2)}) %collective-permute-start.17) | collective-permute-done | bytes 3488 | tf_op jit(solution)/shard_map/ppermute | solution.py:20
  43.0 0.3 pad_maximum_fusion.15
  43.3 0.6 fusion.36
  44.0 1.6 collective-permute-start.2
  45.5 1.3 collective-permute-start.3
  46.8 2.2 %fusion.9 = f32[1,64,64,128]{3,2,1,0:T(8,128)} fusion(f32[64,64,128]{2,1,0:T(8,128)S(1)} %get-tuple-element.9, f32[2,64,128]{2,1,0:T(8,128)S(1)} %collective-permute-done.1, f32[2,64,128]{2,1,0:T(8,128)S(1)} %collective-permute-done), kind=kLoop, calls=%fused_computation.17 | loop fusion | flops 5242880 | bytes 4325376 | tf_op jit(solution)/shard_map/stack | solution.py:94
  49.0 2.7 %collective-permute-done.3 = f32[68,2,128]{2,1,0:T(2,128)S(1)} collective-permute-done((f32[68,2,128]{2,1,0:T(2,128)S(1)}, f32[68,2,128]{2,1,0:T(2,128)S(1)}, u32[]{:S(2)}, u32[]{:S(2)}) %collective-permute-start.3) | collective-permute-done | bytes 69664 | tf_op jit(solution)/shard_map/ppermute | solution.py:20
  51.7 0.4 pad_maximum_fusion.1
  52.1 3.0 %fusion.238 = (f32[68,68,2]{2,1,0:T(8,128)}, f32[68,68,2]{2,1,0:T(8,128)}) fusion(f32[68,68,128]{2,1,0:T(8,128)S(1)} %pad_maximum_fusion.1), kind=kLoop, calls=%fused_computation.304 | loop fusion | bytes 147968 | tf_op jit(solution)/shard_map/slice | solution.py:18
  55.1 2.6 %copy.19 = f32[68,68,2]{1,0,2:T(8,128)S(1)} copy(f32[68,68,2]{2,1,0:T(8,128)} %get-tuple-element.11) | data formatting | bytes 73984 | tf_op jit(solution)/shard_map/slice | solution.py:20
  57.7 1.3 collective-permute-start.5
  59.0 2.6 %copy.17 = f32[68,68,2]{1,2,0:T(2,128)S(1)} copy(f32[68,68,2]{2,1,0:T(8,128)} %get-tuple-element.10) | data formatting | bytes 73984 | tf_op jit(solution)/shard_map/slice | solution.py:18
  61.6 4.6 %collective-permute-start.4 = (f32[68,68,2]{1,2,0:T(2,128)S(1)}, f32[68,68,2]{1,2,0:T(2,128)S(1)}, u32[]{:S(2)}, u32[]{:S(2)}) collective-permute-start(f32[68,68,2]{1,2,0:T(2,128)S(1)} %copy.17), channel_id=1, source_target_pairs={{0,1},{1,2},{2,3},{4,5},{5,6},{6,7},{8,9},{9,10},{10,11},{12,13},{... | collective-permute-start | bytes 110984 | tf_op jit(solution)/shard_map/ppermute | solution.py:17
  66.2 0.4 maximum_maximum_fusion
  66.6 2.1 %fusion.19 = f32[1,64,64,128]{3,2,1,0:T(8,128)} fusion(f32[68,66,128]{2,1,0:T(8,128)S(1)} %get-tuple-element.13, f32[68,66,128]{2,1,0:T(8,128)S(1)} %get-tuple-element.12), kind=kLoop, calls=%fused_computation.39 | loop fusion | flops 3145728 | bytes 10485760 | tf_op jit(solution)/shard_map/stack | solution.py:94
  68.8 2.4 %copy.20 = f32[68,68,2]{2,1,0:T(8,128)} copy(f32[68,68,2]{1,0,2:T(8,128)S(1)} %collective-permute-done.5) | data formatting | bytes 73984 | tf_op jit(solution)/shard_map/ppermute | solution.py:20
  71.1 2.4 %copy.18 = f32[68,68,2]{2,1,0:T(8,128)} copy(f32[68,68,2]{1,2,0:T(2,128)S(1)} %collective-permute-done.4) | data formatting | bytes 73984 | tf_op jit(solution)/shard_map/ppermute | solution.py:17
  73.5 10.4 %fusion.14 = f32[1,64,64,128]{3,2,1,0:T(8,128)S(1)} fusion(f32[68,68,2]{2,1,0:T(8,128)} %copy.20, f32[68,2,128]{2,1,0:T(2,128)S(1)} %collective-permute-done.3, f32[68,2,128]{2,1,0:T(2,128)S(1)} %collective-permute-done.2, f32[2,64,128]{2,1,0:T(8,128)S(1)} %collective-permute-done.1, f32[64,64,128]{2,1,0:T(8,128)S(1)} %get-tuple-element.9, ...), kind=kLoop, calls=%fused_computation.23 | loop fusion | flops 13631488 | bytes 4538624 | tf_op jit(solution)/shard_map/stack | solution.py:94
  83.9 1.1 maximum_multiply_fusion
  85.0 6.5 %fusion.23 = f32[3,12,64,128]{3,1,2,0:T(8,128)S(1)} fusion(f32[3,64,64,128]{3,2,1,0:T(8,128)S(1)} %maximum_multiply_fusion, f32[12]{0:T(128)S(1)} %multiply_add_fusion.4, f32[64]{0:T(128)S(1)} %convert_add_fusion.4), kind=kOutput, calls=%fused_computation.47 | convolution fusion | flops 226506240 | bytes 7471408 | tf_op jit(solution)/shard_map/axyz,xp->apyz/dot_general | solution.py:68
  91.4 1.0 fusion.31
  92.4 0.5 fusion.65
  92.9 1.3 collective-permute-start.6
  94.2 1.5 collective-permute-start.7
  95.7 6.5 %fusion.26 = f32[3,8,64,128]{3,1,2,0:T(8,128)S(1)} fusion(f32[3,64,64,128]{3,2,1,0:T(8,128)S(1)} %maximum_multiply_fusion, f32[8]{0:T(128)S(1)} %multiply_add_fusion.1, f32[64]{0:T(128)S(1)} %convert_add_fusion.1), kind=kOutput, calls=%fused_computation.48 | convolution fusion | flops 151004160 | bytes 7078176 | tf_op jit(solution)/shard_map/axyz,xp->apyz/dot_general | solution.py:68
  102.2 0.6 convolution_bitcast_fusion
  102.9 1.8 %collective-permute-start.8 = (f32[3,8,2,20]{3,2,1,0:T(2,128)S(1)}, f32[3,8,2,20]{3,2,1,0:T(2,128)S(1)}, u32[]{:S(2)}, u32[]{:S(2)}) collective-permute-start(f32[3,8,2,20]{3,2,1,0:T(2,128)S(1)} %get-tuple-element.22), channel_id=1, source_target_pairs={{0,4},{1,5},{2,6},{3,7},{8,12},{9,13},{10,14},{11,15},{16,20},{17,... | collective-permute-start | bytes 11528 | tf_op jit(solution)/shard_map/ppermute | solution.py:17
  104.7 1.3 collective-permute-start.9
  106.0 0.2 fusion.60
  106.2 42.9 %psum.7 = f32[3,8,4,16]{3,1,2,0:T(8,128)S(1)} all-reduce(f32[3,8,4,16]{3,1,2,0:T(8,128)S(1)} %fusion.60), channel_id=1, replica_groups=mesh['gx'=4,'gy'=2,'gz'=4] {'gx','gy','gz'}, use_global_device_ids=true, to_apply=%region_0.1 | all-reduce | flops 1536 | bytes 12288 | tf_op jit(solution)/shard_map/psum | solution.py:119
  149.3 2.2 %collective-permute-start.10 = (f32[3,8,8,2]{3,2,1,0:T(8,128)S(1)}, f32[3,8,8,2]{3,2,1,0:T(8,128)S(1)}, u32[]{:S(2)}, u32[]{:S(2)}) collective-permute-start(f32[3,8,8,2]{3,2,1,0:T(8,128)S(1)} %get-tuple-element.26), channel_id=1, source_target_pairs={{0,1},{1,2},{2,3},{4,5},{5,6},{6,7},{8,9},{9,10},{10,11},{12,13},{... | collective-permute-start | bytes 4616 | tf_op jit(solution)/shard_map/ppermute | solution.py:17
  151.5 1.3 collective-permute-start.11
  152.9 0.6 copy.28
  153.7 4.3 %collective-permute-done.11 = f32[3,8,8,2]{3,2,1,0:T(8,128)S(1)} collective-permute-done((f32[3,8,8,2]{3,2,1,0:T(8,128)S(1)}, f32[3,8,8,2]{3,2,1,0:T(8,128)S(1)}, u32[]{:S(2)}, u32[]{:S(2)}) %collective-permute-start.11) | collective-permute-done | bytes 1568 | tf_op jit(solution)/shard_map/ppermute | solution.py:20
  158.0 0.9 fusion.42
  (52 shorter events, 1.1 us)
Async XLA Ops:
  0.6 8.2 %copy-start.3 = (f32[3,8,8,16]{3,2,1,0:T(8,128)S(1)}, f32[3,8,8,16]{3,2,1,0:T(8,128)}, u32[]{:S(2)}) copy-start(f32[3,8,8,16]{3,2,1,0:T(8,128)} %param.6) | copy-start | bytes 36868
  0.6 14.7 %copy-start.4 = (f32[3,8,4,16]{3,2,1,0:T(4,128)S(1)}, f32[3,8,4,16]{3,2,1,0:T(4,128)}, u32[]{:S(2)}) copy-start(f32[3,8,4,16]{3,2,1,0:T(4,128)} %param.7) | copy-start | bytes 18436
  5.1 38.8 %collective-permute-start = (f32[2,64,128]{2,1,0:T(8,128)S(1)}, f32[2,64,128]{2,1,0:T(8,128)S(1)}, u32[]{:S(2)}, u32[]{:S(2)}) collective-permute-start(f32[2,64,128]{2,1,0:T(8,128)S(1)} %get-tuple-element.16), channel_id=1, source_target_pairs={{0,8},{8,16},{16,24},{1,9},{9,17},{17,25},{2,10},{10,18},{18,26},{... | collective-permute-start | bytes 196616 | tf_op jit(solution)/shard_map/ppermute | solution.py:17
  7.5 36.4 %collective-permute-start.1 = (f32[2,64,128]{2,1,0:T(8,128)S(1)}, f32[2,64,128]{2,1,0:T(8,128)S(1)}, u32[]{:S(2)}, u32[]{:S(2)}) collective-permute-start(f32[2,64,128]{2,1,0:T(8,128)S(1)} %get-tuple-element.17), channel_id=1, source_target_pairs={{8,0},{16,8},{24,16},{9,1},{17,9},{25,17},{10,2},{18,10},{26,18},{... | collective-permute-start | bytes 196616 | tf_op jit(solution)/shard_map/ppermute | solution.py:20
  8.8 6.9 %collective-permute-start.12 = (f32[3,2,8,16]{3,2,1,0:T(8,128)S(1)}, f32[3,2,8,16]{3,2,1,0:T(8,128)S(1)}, u32[]{:S(2)}, u32[]{:S(2)}) collective-permute-start(f32[3,2,8,16]{3,2,1,0:T(8,128)S(1)} %get-tuple-element.29), channel_id=1, source_target_pairs={{0,8},{8,16},{16,24},{1,9},{9,17},{17,25},{2,10},{10,18},{18,26},{... | collective-permute-start | bytes 9224 | tf_op jit(solution)/shard_map/ppermute | solution.py:17
  14.0 4.3 %collective-permute-start.13 = (f32[3,2,8,16]{3,2,1,0:T(8,128)S(1)}, f32[3,2,8,16]{3,2,1,0:T(8,128)S(1)}, u32[]{:S(2)}, u32[]{:S(2)}) collective-permute-start(f32[3,2,8,16]{3,2,1,0:T(8,128)S(1)} %get-tuple-element.28), channel_id=1, source_target_pairs={{8,0},{16,8},{24,16},{9,1},{17,9},{25,17},{10,2},{18,10},{26,18},{... | collective-permute-start | bytes 9224 | tf_op jit(solution)/shard_map/ppermute | solution.py:20
  18.3 5.0 %collective-permute-start.14 = (f32[3,12,2,16]{3,2,1,0:T(2,128)S(1)}, f32[3,12,2,16]{3,2,1,0:T(2,128)S(1)}, u32[]{:S(2)}, u32[]{:S(2)}) collective-permute-start(f32[3,12,2,16]{3,2,1,0:T(2,128)S(1)} %get-tuple-element.24), channel_id=1, source_target_pairs={{0,4},{1,5},{2,6},{3,7},{8,12},{9,13},{10,14},{11,15},{16,20},{17,... | collective-permute-start | bytes 13832 | tf_op jit(solution)/shard_map/ppermute | solution.py:17
  21.8 5.9 %collective-permute-start.15 = (f32[3,12,2,16]{3,2,1,0:T(2,128)S(1)}, f32[3,12,2,16]{3,2,1,0:T(2,128)S(1)}, u32[]{:S(2)}, u32[]{:S(2)}) collective-permute-start(f32[3,12,2,16]{3,2,1,0:T(2,128)S(1)} %get-tuple-element.25), channel_id=1, source_target_pairs={{4,0},{5,1},{6,2},{7,3},{12,8},{13,9},{14,10},{15,11},{20,16},{21,... | collective-permute-start | bytes 13832 | tf_op jit(solution)/shard_map/ppermute | solution.py:20
  27.8 10.7 %collective-permute-start.16 = (f32[3,12,12,2]{3,2,1,0:T(8,128)S(1)}, f32[3,12,12,2]{3,2,1,0:T(8,128)S(1)}, u32[]{:S(2)}, u32[]{:S(2)}) collective-permute-start(f32[3,12,12,2]{3,2,1,0:T(8,128)S(1)} %get-tuple-element.20), channel_id=1, source_target_pairs={{0,1},{1,2},{2,3},{4,5},{5,6},{6,7},{8,9},{9,10},{10,11},{12,13},{... | collective-permute-start | bytes 10376 | tf_op jit(solution)/shard_map/ppermute | solution.py:17
  31.3 11.7 %collective-permute-start.17 = (f32[3,12,12,2]{3,2,1,0:T(8,128)S(1)}, f32[3,12,12,2]{3,2,1,0:T(8,128)S(1)}, u32[]{:S(2)}, u32[]{:S(2)}) collective-permute-start(f32[3,12,12,2]{3,2,1,0:T(8,128)S(1)} %get-tuple-element.21), channel_id=1, source_target_pairs={{1,0},{2,1},{3,2},{5,4},{6,5},{7,6},{9,8},{10,9},{11,10},{13,12},{... | collective-permute-start | bytes 10376 | tf_op jit(solution)/shard_map/ppermute | solution.py:20
  44.0 5.1 %collective-permute-start.2 = (f32[68,2,128]{2,1,0:T(2,128)S(1)}, f32[68,2,128]{2,1,0:T(2,128)S(1)}, u32[]{:S(2)}, u32[]{:S(2)}) collective-permute-start(f32[68,2,128]{2,1,0:T(2,128)S(1)} %get-tuple-element.14), channel_id=1, source_target_pairs={{0,4},{1,5},{2,6},{3,7},{8,12},{9,13},{10,14},{11,15},{16,20},{17,... | collective-permute-start | bytes 208904 | tf_op jit(solution)/shard_map/ppermute | solution.py:17
  45.5 6.2 %collective-permute-start.3 = (f32[68,2,128]{2,1,0:T(2,128)S(1)}, f32[68,2,128]{2,1,0:T(2,128)S(1)}, u32[]{:S(2)}, u32[]{:S(2)}) collective-permute-start(f32[68,2,128]{2,1,0:T(2,128)S(1)} %get-tuple-element.15), channel_id=1, source_target_pairs={{4,0},{5,1},{6,2},{7,3},{12,8},{13,9},{14,10},{15,11},{20,16},{21,... | collective-permute-start | bytes 208904 | tf_op jit(solution)/shard_map/ppermute | solution.py:20
  57.7 11.0 %collective-permute-start.5 = (f32[68,68,2]{1,0,2:T(8,128)S(1)}, f32[68,68,2]{1,0,2:T(8,128)S(1)}, u32[]{:S(2)}, u32[]{:S(2)}) collective-permute-start(f32[68,68,2]{1,0,2:T(8,128)S(1)} %copy.19), channel_id=1, source_target_pairs={{1,0},{2,1},{3,2},{5,4},{6,5},{7,6},{9,8},{10,9},{11,10},{13,12},{... | collective-permute-start | bytes 110984 | tf_op jit(solution)/shard_map/ppermute | solution.py:20
  61.6 9.5 %collective-permute-start.4 = (f32[68,68,2]{1,2,0:T(2,128)S(1)}, f32[68,68,2]{1,2,0:T(2,128)S(1)}, u32[]{:S(2)}, u32[]{:S(2)}) collective-permute-start(f32[68,68,2]{1,2,0:T(2,128)S(1)} %copy.17), channel_id=1, source_target_pairs={{0,1},{1,2},{2,3},{4,5},{5,6},{6,7},{8,9},{9,10},{10,11},{12,13},{... | collective-permute-start | bytes 110984 | tf_op jit(solution)/shard_map/ppermute | solution.py:17
  73.5 10.4 %copy-start = (f32[1,64,64,128]{3,2,1,0:T(8,128)S(1)}, f32[1,64,64,128]{3,2,1,0:T(8,128)}, u32[]{:S(2)}) copy-start(f32[1,64,64,128]{3,2,1,0:T(8,128)} %fusion.19) | copy-start | bytes 6291460
  73.5 10.4 %copy-start.1 = (f32[1,64,64,128]{3,2,1,0:T(8,128)S(1)}, f32[1,64,64,128]{3,2,1,0:T(8,128)}, u32[]{:S(2)}) copy-start(f32[1,64,64,128]{3,2,1,0:T(8,128)} %fusion.9) | copy-start | bytes 6291460
  73.5 10.4 %copy-start.2 = (f32[64,64,128]{2,1,0:T(8,128)S(1)}, f32[64,64,128]{2,1,0:T(8,128)}, u32[]{:S(2)}) copy-start(f32[64,64,128]{2,1,0:T(8,128)} %get-tuple-element.8) | copy-start | bytes 6291460
  92.9 9.9 %collective-permute-start.6 = (f32[3,2,12,20]{3,2,1,0:T(8,128)S(1)}, f32[3,2,12,20]{3,2,1,0:T(8,128)S(1)}, u32[]{:S(2)}, u32[]{:S(2)}) collective-permute-start(f32[3,2,12,20]{3,2,1,0:T(8,128)S(1)} %get-tuple-element.18), channel_id=1, source_target_pairs={{0,8},{8,16},{16,24},{1,9},{9,17},{17,25},{2,10},{10,18},{18,26},{... | collective-permute-start | bytes 17288 | tf_op jit(solution)/shard_map/ppermute | solution.py:17
  94.2 8.6 %collective-permute-start.7 = (f32[3,2,12,20]{3,2,1,0:T(8,128)S(1)}, f32[3,2,12,20]{3,2,1,0:T(8,128)S(1)}, u32[]{:S(2)}, u32[]{:S(2)}) collective-permute-start(f32[3,2,12,20]{3,2,1,0:T(8,128)S(1)} %get-tuple-element.19), channel_id=1, source_target_pairs={{8,0},{16,8},{24,16},{9,1},{17,9},{25,17},{10,2},{18,10},{26,18},{... | collective-permute-start | bytes 17288 | tf_op jit(solution)/shard_map/ppermute | solution.py:20
  102.9 46.3 %collective-permute-start.8 = (f32[3,8,2,20]{3,2,1,0:T(2,128)S(1)}, f32[3,8,2,20]{3,2,1,0:T(2,128)S(1)}, u32[]{:S(2)}, u32[]{:S(2)}) collective-permute-start(f32[3,8,2,20]{3,2,1,0:T(2,128)S(1)} %get-tuple-element.22), channel_id=1, source_target_pairs={{0,4},{1,5},{2,6},{3,7},{8,12},{9,13},{10,14},{11,15},{16,20},{17,... | collective-permute-start | bytes 11528 | tf_op jit(solution)/shard_map/ppermute | solution.py:17
  104.7 44.5 %collective-permute-start.9 = (f32[3,8,2,20]{3,2,1,0:T(2,128)S(1)}, f32[3,8,2,20]{3,2,1,0:T(2,128)S(1)}, u32[]{:S(2)}, u32[]{:S(2)}) collective-permute-start(f32[3,8,2,20]{3,2,1,0:T(2,128)S(1)} %get-tuple-element.23), channel_id=1, source_target_pairs={{4,0},{5,1},{6,2},{7,3},{12,8},{13,9},{14,10},{15,11},{20,16},{21,... | collective-permute-start | bytes 11528 | tf_op jit(solution)/shard_map/ppermute | solution.py:20
  149.3 4.4 %collective-permute-start.10 = (f32[3,8,8,2]{3,2,1,0:T(8,128)S(1)}, f32[3,8,8,2]{3,2,1,0:T(8,128)S(1)}, u32[]{:S(2)}, u32[]{:S(2)}) collective-permute-start(f32[3,8,8,2]{3,2,1,0:T(8,128)S(1)} %get-tuple-element.26), channel_id=1, source_target_pairs={{0,1},{1,2},{2,3},{4,5},{5,6},{6,7},{8,9},{9,10},{10,11},{12,13},{... | collective-permute-start | bytes 4616 | tf_op jit(solution)/shard_map/ppermute | solution.py:17
  151.5 6.5 %collective-permute-start.11 = (f32[3,8,8,2]{3,2,1,0:T(8,128)S(1)}, f32[3,8,8,2]{3,2,1,0:T(8,128)S(1)}, u32[]{:S(2)}, u32[]{:S(2)}) collective-permute-start(f32[3,8,8,2]{3,2,1,0:T(8,128)S(1)} %get-tuple-element.27), channel_id=1, source_target_pairs={{1,0},{2,1},{3,2},{5,4},{6,5},{7,6},{9,8},{10,9},{11,10},{13,12},{... | collective-permute-start | bytes 4616 | tf_op jit(solution)/shard_map/ppermute | solution.py:20
where the time goes:
time: 160 us; the launch traced here: 159 us
  blocking collectives  42.9 us (27%)
  starting transfers between devices  37.7 us (24%)
  waiting for transfers between devices  24.6 us (15%)
  other arithmetic  23.4 us (15%)
  matrix products  15.2 us (10%)
  local copies, waits for them, and re-layouts  13.9 us (9%)
    psum x1, blocking collectives, per_device(): coarse_sum = lax.psum(coarse_part, ('gx', 'gy', 'gz'))  42.9 us
    ppermute x9, starting transfers between devices, padded_2(): lax.ppermute(lax.slice_in_dim(block, block.shape[dim] - width, None, axis...  25.9 us
    ppermute x9, waiting for transfers between devices, padded_2(): lax.ppermute(lax.slice_in_dim(block, 0, width, axis=dim), axis, backward)  18.3 us
    another operation x3, other arithmetic, per_device(): force = jnp.stack(slopes) * difference[None]  14.7 us
    dot_general x2, matrix products, project(): section = jnp.einsum('axyz,xp->apyz', force, along_x, precision=highest)  13 us
    ppermute x9, starting transfers between devices, padded_2(): lax.ppermute(lax.slice_in_dim(block, 0, width, axis=dim), axis, backward)  11.9 us
    ppermute x9, waiting for transfers between devices, padded_2(): lax.ppermute(lax.slice_in_dim(block, block.shape[dim] - width, None, axis...  6.36 us
    slice x8, local copies, waits for them, and re-layouts, padded_2(): lax.slice_in_dim(block, block.shape[dim] - width, None, axis=dim)  5.86 us
  transfers between devices with their start and end apart: 18, of which 8 were waited for; matrix products, arithmetic and copies ran while one was open for 12% of the time, Pallas kernels for 0%

commit v1 on v0

--- a/solution.py
+++ b/solution.py
@@ -116,7 +116,8 @@
     coarse_y = basis_matrix(size_y, coarse_control.shape[2], SPC, lax.axis_index("gy") * size_y, 0)
     coarse_z = basis_matrix(size_z, coarse_control.shape[3], SPC, lax.axis_index("gz") * size_z, 0)
     coarse_part = project(force, coarse_x, coarse_y, coarse_z)
-    coarse_sum = lax.psum(coarse_part, ("gx", "gy", "gz"))
+    blocks = lax.all_gather(coarse_part, ("gx", "gy", "gz"))
+    coarse_sum = jnp.sum(blocks, axis=0)
     coarse_gradient = coarse_sum * SPC ** (-1.5) + bend_factor * laplace(laplace(coarse_control))
     return (fine_gradient, coarse_gradient)
 

time: 160 us -> 200 us (1.25)
  blocking collectives: 42.9 us -> 83.2 us
    all_gather x0 -> x1, blocking collectives: none -> 83.2 us  [per_device(): blocks = lax.all_gather(coarse_part, ('gx', 'gy', 'gz'))]
    psum x1 -> x0, blocking collectives: 42.9 us -> none  [per_device(): coarse_sum = lax.psum(coarse_part, ('gx', 'gy', 'gz'))]
  transfers between devices with their start and end apart: 18 -> 18, of which waited for: 8 -> 8; matrix products, arithmetic and copies ran while one was open for 12% -> 10% of each run, Pallas kernels for 0% -> 0%
where the time goes in v1:
time: 200 us; the launch traced here: 199 us
  blocking collectives  83.2 us (42%)
  starting transfers between devices  37.9 us (19%)
  waiting for transfers between devices  24.7 us (12%)
  other arithmetic  23.4 us (12%)
  matrix products  15.3 us (8%)
  local copies, waits for them, and re-layouts  13.9 us (7%)
    all_gather x1, blocking collectives, per_device(): blocks = lax.all_gather(coarse_part, ('gx', 'gy', 'gz'))  83.2 us
    ppermute x9, starting transfers between devices, padded_2(): lax.ppermute(lax.slice_in_dim(block, block.shape[dim] - width, None, axis...  26 us
    ppermute x9, waiting for transfers between devices, padded_2(): lax.ppermute(lax.slice_in_dim(block, 0, width, axis=dim), axis, backward)  18.3 us
    another operation x3, other arithmetic, per_device(): force = jnp.stack(slopes) * difference[None]  14.7 us
    dot_general x2, matrix products, project(): section = jnp.einsum('axyz,xp->apyz', force, along_x, precision=highest)  13 us
    ppermute x9, starting transfers between devices, padded_2(): lax.ppermute(lax.slice_in_dim(block, 0, width, axis=dim), axis, backward)  11.9 us
    ppermute x9, waiting for transfers between devices, padded_2(): lax.ppermute(lax.slice_in_dim(block, block.shape[dim] - width, None, axis...  6.36 us
    slice x8, local copies, waits for them, and re-layouts, padded_2(): lax.slice_in_dim(block, block.shape[dim] - width, None, axis=dim)  5.86 us
  transfers between devices with their start and end apart: 18, of which 8 were waited for; matrix products, arithmetic and copies ran while one was open for 10% of the time, Pallas kernels for 0%

profile of v1, /device:TPU:0, one launch (start us, length us, event | category | flops | bytes accessed | tf_op | source)
XLA Modules:
  0.0 199.4 jit_solution(1244088295266833155)
XLA Ops:
  0.7 4.2 %fusion.237 = (f32[64,64,128]{2,1,0:T(8,128)}, f32[64,64,128]{2,1,0:T(8,128)S(1)}) fusion(f32[64,64,128]{2,1,0:T(8,128)} %param.4, f32[64,64,128]{2,1,0:T(8,128)} %param.5), kind=kLoop, calls=%fused_computation.303 | loop fusion | flops 1048576 | bytes 8388608 | tf_op jit(solution)/shard_map/sub | solution.py:91
  4.9 2.4 %collective-permute-start = (f32[2,64,128]{2,1,0:T(8,128)S(1)}, f32[2,64,128]{2,1,0:T(8,128)S(1)}, u32[]{:S(2)}, u32[]{:S(2)}) collective-permute-start(f32[2,64,128]{2,1,0:T(8,128)S(1)} %get-tuple-element.14), channel_id=1, source_target_pairs={{0,8},{8,16},{16,24},{1,9},{9,17},{17,25},{2,10},{10,18},{18,26},{... | collective-permute-start | bytes 196616 | tf_op jit(solution)/shard_map/ppermute | solution.py:17
  7.3 1.3 collective-permute-start.1
  8.6 5.1 %collective-permute-start.12 = (f32[3,2,8,16]{3,2,1,0:T(8,128)S(1)}, f32[3,2,8,16]{3,2,1,0:T(8,128)S(1)}, u32[]{:S(2)}, u32[]{:S(2)}) collective-permute-start(f32[3,2,8,16]{3,2,1,0:T(8,128)S(1)} %get-tuple-element.27), channel_id=1, source_target_pairs={{0,8},{8,16},{16,24},{1,9},{9,17},{17,25},{2,10},{10,18},{18,26},{... | collective-permute-start | bytes 9224 | tf_op jit(solution)/shard_map/ppermute | solution.py:17
  13.8 1.3 collective-permute-start.13
  15.5 2.6 %collective-permute-done.13 = f32[3,2,8,16]{3,2,1,0:T(8,128)S(1)} collective-permute-done((f32[3,2,8,16]{3,2,1,0:T(8,128)S(1)}, f32[3,2,8,16]{3,2,1,0:T(8,128)S(1)}, u32[]{:S(2)}, u32[]{:S(2)}) %collective-permute-start.13) | collective-permute-done | bytes 3104 | tf_op jit(solution)/shard_map/ppermute | solution.py:20
  18.1 3.4 %collective-permute-start.14 = (f32[3,12,2,16]{3,2,1,0:T(2,128)S(1)}, f32[3,12,2,16]{3,2,1,0:T(2,128)S(1)}, u32[]{:S(2)}, u32[]{:S(2)}) collective-permute-start(f32[3,12,2,16]{3,2,1,0:T(2,128)S(1)} %get-tuple-element.22), channel_id=1, source_target_pairs={{0,4},{1,5},{2,6},{3,7},{8,12},{9,13},{10,14},{11,15},{16,20},{17,... | collective-permute-start | bytes 13832 | tf_op jit(solution)/shard_map/ppermute | solution.py:17
  21.6 1.3 collective-permute-start.15
  22.9 0.3 collective-permute-done.14
  23.2 4.2 %collective-permute-done.15 = f32[3,12,2,16]{3,2,1,0:T(2,128)S(1)} collective-permute-done((f32[3,12,2,16]{3,2,1,0:T(2,128)S(1)}, f32[3,12,2,16]{3,2,1,0:T(2,128)S(1)}, u32[]{:S(2)}, u32[]{:S(2)}) %collective-permute-start.15) | collective-permute-done | bytes 4640 | tf_op jit(solution)/shard_map/ppermute | solution.py:20
  27.6 3.5 %collective-permute-start.16 = (f32[3,12,12,2]{3,2,1,0:T(8,128)S(1)}, f32[3,12,12,2]{3,2,1,0:T(8,128)S(1)}, u32[]{:S(2)}, u32[]{:S(2)}) collective-permute-start(f32[3,12,12,2]{3,2,1,0:T(8,128)S(1)} %get-tuple-element.18), channel_id=1, source_target_pairs={{0,1},{1,2},{2,3},{4,5},{5,6},{6,7},{8,9},{9,10},{10,11},{12,13},{... | collective-permute-start | bytes 10376 | tf_op jit(solution)/shard_map/ppermute | solution.py:17
  31.1 1.3 collective-permute-start.17
  32.5 5.9 %collective-permute-done.16 = f32[3,12,12,2]{3,2,1,0:T(8,128)S(1)} collective-permute-done((f32[3,12,12,2]{3,2,1,0:T(8,128)S(1)}, f32[3,12,12,2]{3,2,1,0:T(8,128)S(1)}, u32[]{:S(2)}, u32[]{:S(2)}) %collective-permute-start.16) | collective-permute-done | bytes 3488 | tf_op jit(solution)/shard_map/ppermute | solution.py:17
  38.3 4.4 %collective-permute-done.17 = f32[3,12,12,2]{3,2,1,0:T(8,128)S(1)} collective-permute-done((f32[3,12,12,2]{3,2,1,0:T(8,128)S(1)}, f32[3,12,12,2]{3,2,1,0:T(8,128)S(1)}, u32[]{:S(2)}, u32[]{:S(2)}) %collective-permute-start.17) | collective-permute-done | bytes 3488 | tf_op jit(solution)/shard_map/ppermute | solution.py:20
  42.8 0.3 pad_maximum_fusion.15
  43.1 0.6 fusion.36
  43.8 1.6 collective-permute-start.2
  45.3 1.3 collective-permute-start.3
  46.6 2.2 %fusion.9 = f32[1,64,64,128]{3,2,1,0:T(8,128)} fusion(f32[64,64,128]{2,1,0:T(8,128)S(1)} %get-tuple-element.7, f32[2,64,128]{2,1,0:T(8,128)S(1)} %collective-permute-done.1, f32[2,64,128]{2,1,0:T(8,128)S(1)} %collective-permute-done), kind=kLoop, calls=%fused_computation.17 | loop fusion | flops 5242880 | bytes 4325376 | tf_op jit(solution)/shard_map/stack | solution.py:94
  48.8 2.7 %collective-permute-done.3 = f32[68,2,128]{2,1,0:T(2,128)S(1)} collective-permute-done((f32[68,2,128]{2,1,0:T(2,128)S(1)}, f32[68,2,128]{2,1,0:T(2,128)S(1)}, u32[]{:S(2)}, u32[]{:S(2)}) %collective-permute-start.3) | collective-permute-done | bytes 69664 | tf_op jit(solution)/shard_map/ppermute | solution.py:20
  51.5 0.4 pad_maximum_fusion.1
  51.9 3.0 %fusion.238 = (f32[68,68,2]{2,1,0:T(8,128)}, f32[68,68,2]{2,1,0:T(8,128)}) fusion(f32[68,68,128]{2,1,0:T(8,128)S(1)} %pad_maximum_fusion.1), kind=kLoop, calls=%fused_computation.304 | loop fusion | bytes 147968 | tf_op jit(solution)/shard_map/slice | solution.py:18
  54.9 2.6 %copy.16 = f32[68,68,2]{1,0,2:T(8,128)S(1)} copy(f32[68,68,2]{2,1,0:T(8,128)} %get-tuple-element.9) | data formatting | bytes 73984 | tf_op jit(solution)/shard_map/slice | solution.py:20
  57.5 1.3 collective-permute-start.5
  58.8 2.6 %copy.14 = f32[68,68,2]{1,2,0:T(2,128)S(1)} copy(f32[68,68,2]{2,1,0:T(8,128)} %get-tuple-element.8) | data formatting | bytes 73984 | tf_op jit(solution)/shard_map/slice | solution.py:18
  61.4 4.6 %collective-permute-start.4 = (f32[68,68,2]{1,2,0:T(2,128)S(1)}, f32[68,68,2]{1,2,0:T(2,128)S(1)}, u32[]{:S(2)}, u32[]{:S(2)}) collective-permute-start(f32[68,68,2]{1,2,0:T(2,128)S(1)} %copy.14), channel_id=1, source_target_pairs={{0,1},{1,2},{2,3},{4,5},{5,6},{6,7},{8,9},{9,10},{10,11},{12,13},{... | collective-permute-start | bytes 110984 | tf_op jit(solution)/shard_map/ppermute | solution.py:17
  66.0 0.4 maximum_maximum_fusion
  66.4 2.1 %fusion.19 = f32[1,64,64,128]{3,2,1,0:T(8,128)} fusion(f32[68,66,128]{2,1,0:T(8,128)S(1)} %get-tuple-element.11, f32[68,66,128]{2,1,0:T(8,128)S(1)} %get-tuple-element.10), kind=kLoop, calls=%fused_computation.39 | loop fusion | flops 3145728 | bytes 10485760 | tf_op jit(solution)/shard_map/stack | solution.py:94
  68.6 2.4 %copy.17 = f32[68,68,2]{2,1,0:T(8,128)} copy(f32[68,68,2]{1,0,2:T(8,128)S(1)} %collective-permute-done.5) | data formatting | bytes 73984 | tf_op jit(solution)/shard_map/ppermute | solution.py:20
  70.9 2.4 %copy.15 = f32[68,68,2]{2,1,0:T(8,128)} copy(f32[68,68,2]{1,2,0:T(2,128)S(1)} %collective-permute-done.4) | data formatting | bytes 73984 | tf_op jit(solution)/shard_map/ppermute | solution.py:17
  73.3 10.4 %fusion.14 = f32[1,64,64,128]{3,2,1,0:T(8,128)S(1)} fusion(f32[68,68,2]{2,1,0:T(8,128)} %copy.17, f32[68,2,128]{2,1,0:T(2,128)S(1)} %collective-permute-done.3, f32[68,2,128]{2,1,0:T(2,128)S(1)} %collective-permute-done.2, f32[2,64,128]{2,1,0:T(8,128)S(1)} %collective-permute-done.1, f32[64,64,128]{2,1,0:T(8,128)S(1)} %get-tuple-element.7, ...), kind=kLoop, calls=%fused_computation.23 | loop fusion | flops 13631488 | bytes 4538624 | tf_op jit(solution)/shard_map/stack | solution.py:94
  83.7 1.1 maximum_multiply_fusion
  84.8 6.5 %fusion.23 = f32[3,12,64,128]{3,1,2,0:T(8,128)S(1)} fusion(f32[3,64,64,128]{3,2,1,0:T(8,128)S(1)} %maximum_multiply_fusion, f32[12]{0:T(128)S(1)} %multiply_add_fusion.4, f32[64]{0:T(128)S(1)} %convert_add_fusion.4), kind=kOutput, calls=%fused_computation.47 | convolution fusion | flops 226506240 | bytes 7471408 | tf_op jit(solution)/shard_map/axyz,xp->apyz/dot_general | solution.py:68
  91.3 1.0 fusion.31
  92.3 0.5 fusion.65
  92.8 1.3 collective-permute-start.6
  94.1 1.5 collective-permute-start.7
  95.6 6.5 %fusion.26 = f32[3,8,64,128]{3,1,2,0:T(8,128)S(1)} fusion(f32[3,64,64,128]{3,2,1,0:T(8,128)S(1)} %maximum_multiply_fusion, f32[8]{0:T(128)S(1)} %multiply_add_fusion.1, f32[64]{0:T(128)S(1)} %convert_add_fusion.1), kind=kOutput, calls=%fused_computation.48 | convolution fusion | flops 151004160 | bytes 7078176 | tf_op jit(solution)/shard_map/axyz,xp->apyz/dot_general | solution.py:68
  102.1 0.6 convolution_bitcast_fusion
  102.6 0.3 fusion.60
  103.0 1.8 collective-permute-start.8
  104.8 1.3 collective-permute-start.9
  106.1 83.2 %all-gather = f32[96,8,4,16]{3,1,2,0:T(8,128)S(1)} all-gather(f32[3,8,4,16]{3,1,2,0:T(8,128)S(1)} %fusion.60), channel_id=2, replica_groups=mesh['gx'=4,'gy'=2,'gz'=4] {'gx','gy','gz'}, dimensions={0}, use_global_device_ids=true | all-gather | bytes 202752 | tf_op jit(solution)/shard_map/all_gather | solution.py:119
  189.6 2.4 %collective-permute-start.10 = (f32[3,8,8,2]{3,2,1,0:T(8,128)S(1)}, f32[3,8,8,2]{3,2,1,0:T(8,128)S(1)}, u32[]{:S(2)}, u32[]{:S(2)}) collective-permute-start(f32[3,8,8,2]{3,2,1,0:T(8,128)S(1)} %get-tuple-element.24), channel_id=1, source_target_pairs={{0,1},{1,2},{2,3},{4,5},{5,6},{6,7},{8,9},{9,10},{10,11},{12,13},{... | collective-permute-start | bytes 4616 | tf_op jit(solution)/shard_map/ppermute | solution.py:17
  192.0 1.3 collective-permute-start.11
  193.4 0.6 copy.25
  194.2 4.3 %collective-permute-done.11 = f32[3,8,8,2]{3,2,1,0:T(8,128)S(1)} collective-permute-done((f32[3,8,8,2]{3,2,1,0:T(8,128)S(1)}, f32[3,8,8,2]{3,2,1,0:T(8,128)S(1)}, u32[]{:S(2)}, u32[]{:S(2)}) %collective-permute-start.11) | collective-permute-done | bytes 1568 | tf_op jit(solution)/shard_map/ppermute | solution.py:20
  198.5 0.9 fusion.42
  (53 shorter events, 1.3 us)
Async XLA Ops:
  0.6 8.0 %copy-start.3 = (f32[3,8,8,16]{3,2,1,0:T(8,128)S(1)}, f32[3,8,8,16]{3,2,1,0:T(8,128)}, u32[]{:S(2)}) copy-start(f32[3,8,8,16]{3,2,1,0:T(8,128)} %param.6) | copy-start | bytes 36868
  0.6 14.5 %copy-start.4 = (f32[3,8,4,16]{3,2,1,0:T(4,128)S(1)}, f32[3,8,4,16]{3,2,1,0:T(4,128)}, u32[]{:S(2)}) copy-start(f32[3,8,4,16]{3,2,1,0:T(4,128)} %param.7) | copy-start | bytes 18436
  4.9 38.8 %collective-permute-start = (f32[2,64,128]{2,1,0:T(8,128)S(1)}, f32[2,64,128]{2,1,0:T(8,128)S(1)}, u32[]{:S(2)}, u32[]{:S(2)}) collective-permute-start(f32[2,64,128]{2,1,0:T(8,128)S(1)} %get-tuple-element.14), channel_id=1, source_target_pairs={{0,8},{8,16},{16,24},{1,9},{9,17},{17,25},{2,10},{10,18},{18,26},{... | collective-permute-start | bytes 196616 | tf_op jit(solution)/shard_map/ppermute | solution.py:17
  7.3 36.4 %collective-permute-start.1 = (f32[2,64,128]{2,1,0:T(8,128)S(1)}, f32[2,64,128]{2,1,0:T(8,128)S(1)}, u32[]{:S(2)}, u32[]{:S(2)}) collective-permute-start(f32[2,64,128]{2,1,0:T(8,128)S(1)} %get-tuple-element.15), channel_id=1, source_target_pairs={{8,0},{16,8},{24,16},{9,1},{17,9},{25,17},{10,2},{18,10},{26,18},{... | collective-permute-start | bytes 196616 | tf_op jit(solution)/shard_map/ppermute | solution.py:20
  8.6 6.9 %collective-permute-start.12 = (f32[3,2,8,16]{3,2,1,0:T(8,128)S(1)}, f32[3,2,8,16]{3,2,1,0:T(8,128)S(1)}, u32[]{:S(2)}, u32[]{:S(2)}) collective-permute-start(f32[3,2,8,16]{3,2,1,0:T(8,128)S(1)} %get-tuple-element.27), channel_id=1, source_target_pairs={{0,8},{8,16},{16,24},{1,9},{9,17},{17,25},{2,10},{10,18},{18,26},{... | collective-permute-start | bytes 9224 | tf_op jit(solution)/shard_map/ppermute | solution.py:17
  13.8 4.3 %collective-permute-start.13 = (f32[3,2,8,16]{3,2,1,0:T(8,128)S(1)}, f32[3,2,8,16]{3,2,1,0:T(8,128)S(1)}, u32[]{:S(2)}, u32[]{:S(2)}) collective-permute-start(f32[3,2,8,16]{3,2,1,0:T(8,128)S(1)} %get-tuple-element.26), channel_id=1, source_target_pairs={{8,0},{16,8},{24,16},{9,1},{17,9},{25,17},{10,2},{18,10},{26,18},{... | collective-permute-start | bytes 9224 | tf_op jit(solution)/shard_map/ppermute | solution.py:20
  18.1 5.0 %collective-permute-start.14 = (f32[3,12,2,16]{3,2,1,0:T(2,128)S(1)}, f32[3,12,2,16]{3,2,1,0:T(2,128)S(1)}, u32[]{:S(2)}, u32[]{:S(2)}) collective-permute-start(f32[3,12,2,16]{3,2,1,0:T(2,128)S(1)} %get-tuple-element.22), channel_id=1, source_target_pairs={{0,4},{1,5},{2,6},{3,7},{8,12},{9,13},{10,14},{11,15},{16,20},{17,... | collective-permute-start | bytes 13832 | tf_op jit(solution)/shard_map/ppermute | solution.py:17
  21.6 5.9 %collective-permute-start.15 = (f32[3,12,2,16]{3,2,1,0:T(2,128)S(1)}, f32[3,12,2,16]{3,2,1,0:T(2,128)S(1)}, u32[]{:S(2)}, u32[]{:S(2)}) collective-permute-start(f32[3,12,2,16]{3,2,1,0:T(2,128)S(1)} %get-tuple-element.23), channel_id=1, source_target_pairs={{4,0},{5,1},{6,2},{7,3},{12,8},{13,9},{14,10},{15,11},{20,16},{21,... | collective-permute-start | bytes 13832 | tf_op jit(solution)/shard_map/ppermute | solution.py:20
  27.6 10.7 %collective-permute-start.16 = (f32[3,12,12,2]{3,2,1,0:T(8,128)S(1)}, f32[3,12,12,2]{3,2,1,0:T(8,128)S(1)}, u32[]{:S(2)}, u32[]{:S(2)}) collective-permute-start(f32[3,12,12,2]{3,2,1,0:T(8,128)S(1)} %get-tuple-element.18), channel_id=1, source_target_pairs={{0,1},{1,2},{2,3},{4,5},{5,6},{6,7},{8,9},{9,10},{10,11},{12,13},{... | collective-permute-start | bytes 10376 | tf_op jit(solution)/shard_map/ppermute | solution.py:17
  31.1 11.7 %collective-permute-start.17 = (f32[3,12,12,2]{3,2,1,0:T(8,128)S(1)}, f32[3,12,12,2]{3,2,1,0:T(8,128)S(1)}, u32[]{:S(2)}, u32[]{:S(2)}) collective-permute-start(f32[3,12,12,2]{3,2,1,0:T(8,128)S(1)} %get-tuple-element.19), channel_id=1, source_target_pairs={{1,0},{2,1},{3,2},{5,4},{6,5},{7,6},{9,8},{10,9},{11,10},{13,12},{... | collective-permute-start | bytes 10376 | tf_op jit(solution)/shard_map/ppermute | solution.py:20
  43.8 5.0 %collective-permute-start.2 = (f32[68,2,128]{2,1,0:T(2,128)S(1)}, f32[68,2,128]{2,1,0:T(2,128)S(1)}, u32[]{:S(2)}, u32[]{:S(2)}) collective-permute-start(f32[68,2,128]{2,1,0:T(2,128)S(1)} %get-tuple-element.12), channel_id=1, source_target_pairs={{0,4},{1,5},{2,6},{3,7},{8,12},{9,13},{10,14},{11,15},{16,20},{17,... | collective-permute-start | bytes 208904 | tf_op jit(solution)/shard_map/ppermute | solution.py:17
  45.3 6.2 %collective-permute-start.3 = (f32[68,2,128]{2,1,0:T(2,128)S(1)}, f32[68,2,128]{2,1,0:T(2,128)S(1)}, u32[]{:S(2)}, u32[]{:S(2)}) collective-permute-start(f32[68,2,128]{2,1,0:T(2,128)S(1)} %get-tuple-element.13), channel_id=1, source_target_pairs={{4,0},{5,1},{6,2},{7,3},{12,8},{13,9},{14,10},{15,11},{20,16},{21,... | collective-permute-start | bytes 208904 | tf_op jit(solution)/shard_map/ppermute | solution.py:20
  57.5 11.0 %collective-permute-start.5 = (f32[68,68,2]{1,0,2:T(8,128)S(1)}, f32[68,68,2]{1,0,2:T(8,128)S(1)}, u32[]{:S(2)}, u32[]{:S(2)}) collective-permute-start(f32[68,68,2]{1,0,2:T(8,128)S(1)} %copy.16), channel_id=1, source_target_pairs={{1,0},{2,1},{3,2},{5,4},{6,5},{7,6},{9,8},{10,9},{11,10},{13,12},{... | collective-permute-start | bytes 110984 | tf_op jit(solution)/shard_map/ppermute | solution.py:20
  61.4 9.5 %collective-permute-start.4 = (f32[68,68,2]{1,2,0:T(2,128)S(1)}, f32[68,68,2]{1,2,0:T(2,128)S(1)}, u32[]{:S(2)}, u32[]{:S(2)}) collective-permute-start(f32[68,68,2]{1,2,0:T(2,128)S(1)} %copy.14), channel_id=1, source_target_pairs={{0,1},{1,2},{2,3},{4,5},{5,6},{6,7},{8,9},{9,10},{10,11},{12,13},{... | collective-permute-start | bytes 110984 | tf_op jit(solution)/shard_map/ppermute | solution.py:17
  73.3 10.4 %copy-start = (f32[1,64,64,128]{3,2,1,0:T(8,128)S(1)}, f32[1,64,64,128]{3,2,1,0:T(8,128)}, u32[]{:S(2)}) copy-start(f32[1,64,64,128]{3,2,1,0:T(8,128)} %fusion.19) | copy-start | bytes 6291460
  73.3 10.4 %copy-start.1 = (f32[1,64,64,128]{3,2,1,0:T(8,128)S(1)}, f32[1,64,64,128]{3,2,1,0:T(8,128)}, u32[]{:S(2)}) copy-start(f32[1,64,64,128]{3,2,1,0:T(8,128)} %fusion.9) | copy-start | bytes 6291460
  73.3 10.4 %copy-start.2 = (f32[64,64,128]{2,1,0:T(8,128)S(1)}, f32[64,64,128]{2,1,0:T(8,128)}, u32[]{:S(2)}) copy-start(f32[64,64,128]{2,1,0:T(8,128)} %get-tuple-element.6) | copy-start | bytes 6291460
  92.8 10.1 %collective-permute-start.6 = (f32[3,2,12,20]{3,2,1,0:T(8,128)S(1)}, f32[3,2,12,20]{3,2,1,0:T(8,128)S(1)}, u32[]{:S(2)}, u32[]{:S(2)}) collective-permute-start(f32[3,2,12,20]{3,2,1,0:T(8,128)S(1)} %get-tuple-element.16), channel_id=1, source_target_pairs={{0,8},{8,16},{16,24},{1,9},{9,17},{17,25},{2,10},{10,18},{18,26},{... | collective-permute-start | bytes 17288 | tf_op jit(solution)/shard_map/ppermute | solution.py:17
  94.1 8.9 %collective-permute-start.7 = (f32[3,2,12,20]{3,2,1,0:T(8,128)S(1)}, f32[3,2,12,20]{3,2,1,0:T(8,128)S(1)}, u32[]{:S(2)}, u32[]{:S(2)}) collective-permute-start(f32[3,2,12,20]{3,2,1,0:T(8,128)S(1)} %get-tuple-element.17), channel_id=1, source_target_pairs={{8,0},{16,8},{24,16},{9,1},{17,9},{25,17},{10,2},{18,10},{26,18},{... | collective-permute-start | bytes 17288 | tf_op jit(solution)/shard_map/ppermute | solution.py:20
  103.0 86.5 %collective-permute-start.8 = (f32[3,8,2,20]{3,2,1,0:T(2,128)S(1)}, f32[3,8,2,20]{3,2,1,0:T(2,128)S(1)}, u32[]{:S(2)}, u32[]{:S(2)}) collective-permute-start(f32[3,8,2,20]{3,2,1,0:T(2,128)S(1)} %get-tuple-element.20), channel_id=1, source_target_pairs={{0,4},{1,5},{2,6},{3,7},{8,12},{9,13},{10,14},{11,15},{16,20},{17,... | collective-permute-start | bytes 11528 | tf_op jit(solution)/shard_map/ppermute | solution.py:17
  104.8 84.7 %collective-permute-start.9 = (f32[3,8,2,20]{3,2,1,0:T(2,128)S(1)}, f32[3,8,2,20]{3,2,1,0:T(2,128)S(1)}, u32[]{:S(2)}, u32[]{:S(2)}) collective-permute-start(f32[3,8,2,20]{3,2,1,0:T(2,128)S(1)} %get-tuple-element.21), channel_id=1, source_target_pairs={{4,0},{5,1},{6,2},{7,3},{12,8},{13,9},{14,10},{15,11},{20,16},{21,... | collective-permute-start | bytes 11528 | tf_op jit(solution)/shard_map/ppermute | solution.py:20
  189.6 4.6 %collective-permute-start.10 = (f32[3,8,8,2]{3,2,1,0:T(8,128)S(1)}, f32[3,8,8,2]{3,2,1,0:T(8,128)S(1)}, u32[]{:S(2)}, u32[]{:S(2)}) collective-permute-start(f32[3,8,8,2]{3,2,1,0:T(8,128)S(1)} %get-tuple-element.24), channel_id=1, source_target_pairs={{0,1},{1,2},{2,3},{4,5},{5,6},{6,7},{8,9},{9,10},{10,11},{12,13},{... | collective-permute-start | bytes 4616 | tf_op jit(solution)/shard_map/ppermute | solution.py:17
  192.0 6.5 %collective-permute-start.11 = (f32[3,8,8,2]{3,2,1,0:T(8,128)S(1)}, f32[3,8,8,2]{3,2,1,0:T(8,128)S(1)}, u32[]{:S(2)}, u32[]{:S(2)}) collective-permute-start(f32[3,8,8,2]{3,2,1,0:T(8,128)S(1)} %get-tuple-element.25), channel_id=1, source_target_pairs={{1,0},{2,1},{3,2},{5,4},{6,5},{7,6},{9,8},{10,9},{11,10},{13,12},{... | collective-permute-start | bytes 4616 | tf_op jit(solution)/shard_map/ppermute | solution.py:20
